TPU v7x, 256 devices: a whole 4x4x8 slice. The times are simulated.
256 devices in a mesh: mrow: 8 (over y, z_lo), pcol: 32 (over x, z_hi, core).
Axes of the slice: x: 4, y: 4, z: 8 (z_hi: 4, z_lo: 2; z = z_hi * 2 + z_lo), core: 2. Of those that a mesh axis runs over, the one named last changes fastest.
Arguments:
- snapshots: bfloat16 [7424, 8192], P('mrow', 'pcol'), may hold values from -16 to 16
- area_weight: float32 [8192], P('pcol'), may hold values from 0.2 to 1
Outputs:
- gram_tiles: float32 [8, 32, 215296], P('mrow', 'pcol')
All inputs are finite; a program needn't handle non-finite values.
Results may differ from a plain program's by a relative error of at most 0.0003.
Values may be sent and summed in bfloat16 or wider, within the bound.
A program may use at most 64 MiB of HBM per device.

v0:
```python
import jax
import jax.numpy as jnp
from jax import lax
from jax.sharding import Mesh
from jax.sharding import PartitionSpec as P

MEMBERS = 7424
MROW = ("mrow_0", "mrow_1")


def sent_to_all(value, axis):
    copies = jnp.broadcast_to(value, (lax.axis_size(axis), *value.shape))
    return lax.all_to_all(copies, axis, split_axis=0, concat_axis=0, tiled=True)


def of_everyone(value, axis):
    everything = sent_to_all(value, axis)
    return jnp.sum(everything, axis=0)


def gather_axes(value, axes, dim):
    for axis in reversed(axes):
        value = lax.all_gather(value, axis, axis=dim, tiled=True)
    return value


def local(snapshots, area_weight):
    member_rows = snapshots.shape[0]
    ratio = lax.axis_size("pcol") // lax.axis_size(MROW)
    tile = member_rows // ratio
    local_sum = jnp.sum(snapshots.astype(jnp.float32), axis=0)
    ens_mean = of_everyone(local_sum, MROW) / MEMBERS
    anomaly = (
        (snapshots.astype(jnp.float32) - ens_mean[None, :]) * jnp.sqrt(area_weight)[None, :]
    ).astype(jnp.bfloat16)
    contract = (((1,), (1,)), ((), ()))
    every_member = gather_axes(anomaly, MROW, 0)
    col_block = lax.all_to_all(every_member, "pcol", split_axis=0, concat_axis=1, tiled=True)
    gram = lax.dot_general(
        lax.all_gather(anomaly, "pcol", axis=1, tiled=True),
        col_block,
        contract,
        preferred_element_type=jnp.float32,
    )
    gram = gram / (MEMBERS - 1)
    return gram.reshape(1, 1, member_rows * tile)


def solution(mesh):
    torus = Mesh(mesh.devices.reshape(4, 2, mesh.shape["pcol"]), ("mrow_0", "mrow_1", "pcol"))
    return jax.shard_map(
        local,
        mesh=torus,
        in_specs=(P(MROW, "pcol"), P("pcol")),
        out_specs=P(MROW, "pcol", None),
        check_vma=False,
    )
```

profile of v0, /device:TPU:1, one launch (start us, length us, event | category | flops | bytes accessed | tf_op | source)
XLA Modules:
  0.0 288.2 jit_solution(7553588986702876311)
XLA Ops:
  6.5 1.2 convert_reduce_fusion
  7.7 0.6 broadcast_in_dim.2
  8.3 6.4 %all-to-all-start = ((f32[8,1,256]{2,1,0:T(1,128)}), f32[8,1,256]{2,1,0:T(1,128)S(1)}, u32[]{:S(2)}, u32[]{:S(2)}) async-start(f32[8,1,256]{2,1,0:T(1,128)} %broadcast_in_dim.2), calls=%async_computation | async-start | bytes 16384 | tf_op jit(solution)/shard_map/all_to_all | solution.py:13
  14.7 0.0 all-gather.5.cloned.1.call-start
  14.7 0.7 sqrt.3
  15.4 4.3 %all-to-all-done = f32[8,1,256]{2,1,0:T(1,128)S(1)} async-done(((f32[8,1,256]{2,1,0:T(1,128)}), f32[8,1,256]{2,1,0:T(1,128)S(1)}, u32[]{:S(2)}, u32[]{:S(2)}) %all-to-all-start) | async-done | bytes 8224 | tf_op jit(solution)/shard_map/all_to_all | solution.py:13
  19.7 1.1 fusion.1
  20.9 0.0 copy-start
  20.9 11.1 %all_gather.10 = bf16[1856,256]{1,0:T(8,128)(2,1)} all-gather(bf16[928,256]{1,0:T(8,128)(2,1)S(1)} %fusion.1), channel_id=1, replica_groups=mesh['mrow_0'=4,'mrow_1'=2,'pcol'=32] {'mrow_1'}, dimensions={0}, use_global_device_ids=true | all-gather | bytes 1425408 | tf_op jit(solution)/shard_map/all_gather | solution.py:23
  32.0 0.0 all-gather.5.cloned.1.call-update
  32.0 0.0 all-gather.3.cloned.1.call-start
  32.1 0.0 copy-done
  32.1 0.7 all-gather.3.cloned.1.call-update
  32.8 49.1 %all-gather.5.cloned.1.call-done = bf16[7424,256]{1,0:T(8,128)(2,1)} async-done(((bf16[1856,256]{1,0:T(8,128)(2,1)}), bf16[7424,256]{1,0:T(8,128)(2,1)}) %all-gather.5.cloned.1.call-update) | async-done | bytes 3801104 | tf_op jit(solution)/shard_map/all_gather | solution.py:23
  81.9 113.8 %all_to_all.25 = bf16[32,232,256]{2,1,0:T(8,128)(2,1)S(1)} all-to-all(bf16[32,232,256]{2,1,0:T(8,128)(2,1)} %bitcast.7), channel_id=1, replica_groups=mesh['mrow_0'=4,'mrow_1'=2,'pcol'=32] {'pcol'}, dimensions={0} | all-to-all | bytes 7602176 | tf_op jit(solution)/shard_map/all_to_all | solution.py:38
  195.7 2.3 copy.9
  198.0 72.2 %all-gather.3.cloned.1.call-done = bf16[928,8192]{1,0:T(8,128)(2,1)} async-done(((bf16[928,256]{1,0:T(8,128)(2,1)}), bf16[928,8192]{1,0:T(8,128)(2,1)}) %all-gather.3.cloned.1.call-update) | async-done | bytes 15204368 | tf_op jit(solution)/shard_map/all_gather | solution.py:40
  270.3 8.6 %convolution_multiply_fusion = f32[928,232]{1,0:T(8,128)S(1)} fusion(bf16[928,8192]{1,0:T(8,128)(2,1)} %all-gather.3.cloned.1.call-done, bf16[232,8192]{1,0:T(8,128)(2,1)} %bitcast.8), kind=kOutput, calls=%fused_computation | convolution fusion | flops 3527624960 | bytes 19866624 | tf_op jit(solution)/shard_map/dot_general | solution.py:39
  278.8 2.6 reshape.14
  (2 shorter events, 0.0 us)
Async XLA Ops:
  8.3 11.4 %all-to-all-start = ((f32[8,1,256]{2,1,0:T(1,128)}), f32[8,1,256]{2,1,0:T(1,128)S(1)}, u32[]{:S(2)}, u32[]{:S(2)}) async-start(f32[8,1,256]{2,1,0:T(1,128)} %broadcast_in_dim.2), calls=%async_computation | async-start | bytes 16384 | tf_op jit(solution)/shard_map/all_to_all | solution.py:13
  14.7 67.2 %all-gather.5.cloned.1.call-start = ((), (), s32[]{:S(2)}) async-start(), calls=%async_computation.3 | async-start | bytes 4751360 | tf_op jit(solution)/shard_map/all_gather | solution.py:23
  20.9 11.2 %copy-start = (bf16[928,256]{1,0:T(8,128)(2,1)}, bf16[928,256]{1,0:T(8,128)(2,1)S(1)}, u32[]{:S(2)}) copy-start(bf16[928,256]{1,0:T(8,128)(2,1)S(1)} %fusion.1) | copy-start | bytes 1425412
  32.0 238.2 %all-gather.3.cloned.1.call-start = ((), (), s32[]{:S(2)}) async-start(), calls=%async_computation.2 | async-start | bytes 15679488 | tf_op jit(solution)/shard_map/all_gather | solution.py:40
Sparse Core Ops, SparseCore 0:
  32.1 49.6 all-gather.4
  84.3 185.8 all-gather.2
where the time goes:
time: 289 us; the launch traced here: 288 us
  waiting for transfers between devices  126 us (44%)
  blocking collectives  125 us (43%)
  between operations  13.4 us (5%)
  matrix products  8.57 us (3%)
  starting transfers between devices  6.44 us (2%)
  local copies, waits for them, and re-layouts  6.17 us (2%)
    all_to_all x1, blocking collectives, local(): lax.all_to_all(every_member, 'pcol', split_axis=0, concat_axis=1, tiled=T...  114 us
    all_gather x1, waiting for transfers between devices, local(): lax.all_gather(anomaly, 'pcol', axis=1, tiled=True)  72.2 us
    all_gather x1, waiting for transfers between devices, gather_axes(): value = lax.all_gather(value, axis, axis=dim, tiled=True)  49.1 us
    all_gather x1, blocking collectives, gather_axes(): value = lax.all_gather(value, axis, axis=dim, tiled=True)  11.1 us
    dot_general x1, matrix products, local(): lax.dot_general(lax.all_gather(anomaly, 'pcol', axis=1, tiled=True), col_...  8.57 us
    all_to_all x1, starting transfers between devices, sent_to_all(): return lax.all_to_all(copies, axis, split_axis=0, concat_axis=0, tiled=True)  6.36 us
  transfers between devices with their start and end apart: 3, of which 3 were waited for; matrix products, arithmetic and copies ran while one was open for 1% of the time, Pallas kernels for 0%

commit v1 on v0

--- a/solution.py
+++ b/solution.py
@@ -37,7 +37,9 @@
     every_member = gather_axes(anomaly, MROW, 0)
     col_block = lax.all_to_all(every_member, "pcol", split_axis=0, concat_axis=1, tiled=True)
     gram = lax.dot_general(
-        lax.all_gather(anomaly, "pcol", axis=1, tiled=True),
+        jnp.concatenate(
+            lax.all_to_all(jnp.stack([anomaly] * lax.axis_size("pcol")), "pcol", 0, 0), axis=1
+        ),
         col_block,
         contract,
         preferred_element_type=jnp.float32,

time: 289 us -> 539 us (1.87)
  blocking collectives: 125 us -> 448 us
  waiting for transfers between devices: 126 us -> 54.2 us
    all_to_all x0 -> x1, blocking collectives: none -> 338 us  [local(): lax.all_to_all(jnp.stack([anomaly] * lax.axis_size('pcol')), 'pcol', 0, 0)]
    all_gather x1 -> x0, waiting for transfers between devices: 72.2 us -> none  [local(): lax.all_gather(anomaly, 'pcol', axis=1, tiled=True)]
    all_to_all x1, blocking collectives: 114 us -> 98.8 us  [local(): lax.all_to_all(every_member, 'pcol', split_axis=0, concat_axis=1, tiled=T...]
    another operation x0 -> x1, local copies, waits for them, and re-layouts: none -> 7.05 us  [local(): jnp.stack([anomaly] * lax.axis_size('pcol'))]
  transfers between devices with their start and end apart: 3 -> 2, of which waited for: 3 -> 2; matrix products, arithmetic and copies ran while one was open for 1% -> 0% of each run, Pallas kernels for 0% -> 0%
where the time goes in v1:
time: 539 us
  blocking collectives  448 us (83%)
  waiting for transfers between devices  54.2 us (10%)
  between operations  13.4 us (2%)
  local copies, waits for them, and re-layouts  10.9 us (2%)
  starting transfers between devices  6.4 us (1%)
    all_to_all x1, blocking collectives, local(): lax.all_to_all(jnp.stack([anomaly] * lax.axis_size('pcol')), 'pcol', 0, 0)  338 us
    all_to_all x1, blocking collectives, local(): lax.all_to_all(every_member, 'pcol', split_axis=0, concat_axis=1, tiled=T...  98.8 us
    all_gather x1, waiting for transfers between devices, gather_axes(): value = lax.all_gather(value, axis, axis=dim, tiled=True)  49.9 us
    all_gather x1, blocking collectives, gather_axes(): value = lax.all_gather(value, axis, axis=dim, tiled=True)  11.1 us
  transfers between devices with their start and end apart: 2, of which 2 were waited for; matrix products, arithmetic and copies ran while one was open for 0% of the time, Pallas kernels for 0%

profile of v1, /device:TPU:1, one launch (start us, length us, event | category | flops | bytes accessed | tf_op | source)
XLA Modules:
  0.0 539.1 jit_solution(11721172851158314472)
XLA Ops:
  6.5 1.2 convert_reduce_fusion
  7.7 0.6 broadcast_in_dim.2
  8.3 6.4 %all-to-all-start = ((f32[8,1,256]{2,1,0:T(1,128)}), f32[8,1,256]{2,1,0:T(1,128)S(1)}, u32[]{:S(2)}, u32[]{:S(2)}) async-start(f32[8,1,256]{2,1,0:T(1,128)} %broadcast_in_dim.2), calls=%async_computation | async-start | bytes 16384 | tf_op jit(solution)/shard_map/all_to_all | solution.py:13
  14.7 0.0 all-gather.2.cloned.1.call-start
  14.7 0.7 sqrt.3
  15.4 4.3 all-to-all-done
  19.7 1.1 fusion.14
  20.9 11.1 %all_gather.6 = bf16[1856,256]{1,0:T(8,128)(2,1)} all-gather(bf16[928,256]{1,0:T(8,128)(2,1)S(1)} %fusion.14), channel_id=1, replica_groups=mesh['mrow_0'=4,'mrow_1'=2,'pcol'=32] {'mrow_1'}, dimensions={0}, use_global_device_ids=true | all-gather | bytes 1425408 | tf_op jit(solution)/shard_map/all_gather | solution.py:23
  32.0 0.0 all-gather.2.cloned.1.call-update
  32.0 49.9 %all-gather.2.cloned.1.call-done = bf16[7424,256]{1,0:T(8,128)(2,1)} async-done(((bf16[1856,256]{1,0:T(8,128)(2,1)}), bf16[7424,256]{1,0:T(8,128)(2,1)}) %all-gather.2.cloned.1.call-update) | async-done | bytes 3801104 | tf_op jit(solution)/shard_map/all_gather | solution.py:23
  81.9 98.8 %all_to_all.27 = bf16[32,232,256]{2,1,0:T(8,128)(2,1)} all-to-all(bf16[32,232,256]{2,1,0:T(8,128)(2,1)} %bitcast.19), channel_id=1, replica_groups=mesh['mrow_0'=4,'mrow_1'=2,'pcol'=32] {'pcol'}, dimensions={0} | all-to-all | bytes 7602176 | tf_op jit(solution)/shard_map/all_to_all | solution.py:38
  180.7 7.1 %stack.2 = bf16[32,928,256]{2,1,0:T(8,128)(2,1)} broadcast(bf16[928,256]{1,0:T(8,128)(2,1)S(1)} %fusion.14), dimensions={1,2} | broadcast | bytes 15679488 | tf_op jit(solution)/shard_map/stack | solution.py:41
  187.7 0.0 copy-start
  187.7 337.9 %all_to_all.28 = bf16[32,928,256]{2,1,0:T(8,128)(2,1)S(1)} all-to-all(bf16[32,928,256]{2,1,0:T(8,128)(2,1)} %stack.2), channel_id=1, replica_groups=mesh['mrow_0'=4,'mrow_1'=2,'pcol'=32] {'pcol'}, dimensions={0} | all-to-all | bytes 30408704 | tf_op jit(solution)/shard_map/all_to_all | solution.py:41
  525.6 0.0 copy-done
  525.6 4.1 fusion.8
  529.7 2.6 reshape.21
  (2 shorter events, 0.0 us)
Async XLA Ops:
  8.3 11.4 %all-to-all-start = ((f32[8,1,256]{2,1,0:T(1,128)}), f32[8,1,256]{2,1,0:T(1,128)S(1)}, u32[]{:S(2)}, u32[]{:S(2)}) async-start(f32[8,1,256]{2,1,0:T(1,128)} %broadcast_in_dim.2), calls=%async_computation | async-start | bytes 16384 | tf_op jit(solution)/shard_map/all_to_all | solution.py:13
  14.7 67.2 %all-gather.2.cloned.1.call-start = ((), (), s32[]{:S(2)}) async-start(), calls=%async_computation.3 | async-start | bytes 4751360 | tf_op jit(solution)/shard_map/all_gather | solution.py:23
  187.7 337.9 %copy-start = (bf16[32,232,256]{2,1,0:T(8,128)(2,1)S(1)}, bf16[32,232,256]{2,1,0:T(8,128)(2,1)}, u32[]{:S(2)}) copy-start(bf16[32,232,256]{2,1,0:T(8,128)(2,1)} %all_to_all.27) | copy-start | bytes 11403268
Sparse Core Ops, SparseCore 0:
  32.1 49.6 all-gather.1
